TPU v7x, 32 devices: a whole 2x2x4 slice. The times are simulated.
32 devices in a mesh: dp: 8 (over z, y), mp: 4 (over x, core).
Axes of the slice: x: 2, y: 2, z: 4, core: 2. Of those that a mesh axis runs over, the one named last changes fastest.
Arguments:
- tokens: bfloat16 [8192, 4096], P('dp', 'mp'), may hold values from -6 to 6
- right_weight: bfloat16 [64, 64, 64], P('mp', 'dp'), may hold values from -0.75 to 0.75
- left_weight: bfloat16 [64, 64, 64], P('mp', 'dp'), may hold values from -0.75 to 0.75
- cotangent: bfloat16 [8192, 4096], P('dp', 'mp'), may hold values from -0.06591797 to 0.06591797
Outputs:
- activated: bfloat16 [8192, 4096], P('dp', 'mp')
- grad_right: float32 [64, 64, 64], P('mp', 'dp')
- grad_left: float32 [64, 64, 64], P('mp', 'dp')
All inputs are finite; a program needn't handle non-finite values.
Results may differ from a plain program's by a relative error of at most 0.0056.
Values may be sent and summed in bfloat16 or wider, within the bound.
A program may use at most 64 MiB of HBM per device.

v0:
```python
import jax
import jax.numpy as jnp
from jax import lax
from jax.sharding import PartitionSpec as P

NB = 64
BS = 64


def gelu_slope(pre):
    cdf = 0.5 * (1.0 + lax.erf(pre * 0.7071067811865476))
    density = jnp.exp(-0.5 * pre * pre) * 0.3989422804014327
    return cdf + pre * density


def shards(tokens, right_weight, left_weight, cotangent):
    tok_rows = tokens.shape[0]
    groups = lax.axis_size("mp")
    owned = NB // groups
    right_rows, left_rows = (
        lax.all_gather(right_weight, "dp", axis=1, tiled=True),
        lax.all_gather(left_weight, "dp", axis=1, tiled=True),
    )
    xs = tokens.reshape(tok_rows, owned, BS)
    inner = jnp.einsum("tik,ikm->tmi", xs, right_rows, preferred_element_type=jnp.float32)
    inner = inner.astype(jnp.bfloat16).reshape(tok_rows, BS * owned)
    left_four = left_rows.reshape(owned, groups, owned, BS)
    received = lax.all_to_all(inner, "mp", split_axis=1, concat_axis=1, tiled=True)
    rows = received.shape[0]
    mixed = received.reshape(rows, groups, owned, owned)
    pre_rows = jnp.einsum("tpmj,mpjn->tmn", mixed, left_four, preferred_element_type=jnp.float32)
    received, pre = (received, pre_rows)
    mixed = received.reshape(tok_rows, groups, owned, owned)
    activated = (
        jax.nn.gelu(pre, approximate=False).astype(jnp.bfloat16).reshape(tok_rows, owned * BS)
    )
    dpre = (cotangent.reshape(tok_rows, owned, BS).astype(jnp.float32) * gelu_slope(pre)).astype(
        jnp.bfloat16
    )
    part_left = jnp.einsum("tpmj,tmn->mpjn", mixed, dpre, preferred_element_type=jnp.float32)
    part_left = part_left.reshape(owned, NB, BS)
    dmixed = jnp.einsum("tmn,mpjn->tpmj", dpre, left_four, preferred_element_type=jnp.float32)
    dmixed = dmixed.astype(jnp.bfloat16).reshape(tok_rows, groups * owned * owned)
    dinner = lax.all_to_all(dmixed, "mp", split_axis=1, concat_axis=1, tiled=True)
    dinner = dinner.reshape(tok_rows, groups, owned, owned)
    part_right = jnp.einsum("tik,tqmi->ikqm", xs, dinner, preferred_element_type=jnp.float32)
    part_right = part_right.reshape(owned, BS, BS)
    grad_right, grad_left = (
        lax.psum_scatter(part_right, "dp", scatter_dimension=1, tiled=True),
        lax.psum_scatter(part_left, "dp", scatter_dimension=1, tiled=True),
    )
    return (activated, grad_right, grad_left)


def solution(mesh):
    return jax.shard_map(
        shards,
        mesh=mesh,
        in_specs=(P("dp", "mp"), P("mp", "dp", None), P("mp", "dp", None), P("dp", "mp")),
        out_specs=(P("dp", "mp"), P("mp", "dp", None), P("mp", "dp", None)),
        check_vma=False,
    )
```

profile of v0, /device:TPU:0, one launch (start us, length us, event | category | flops | bytes accessed | tf_op | source)
XLA Modules:
  0.0 236.4 jit_solution(14564301819312253097)
XLA Ops:
  7.2 28.6 %all_gather.6 = bf16[16,64,64]{2,1,0:T(8,128)(2,1)S(1)} all-gather(bf16[16,8,64]{2,1,0:T(8,128)(2,1)} %param.5), channel_id=1, replica_groups=mesh['dp'=8,'mp'=4] {'dp'}, dimensions={1}, use_global_device_ids=true | all-gather | bytes 147456 | tf_op jit(solution)/shard_map/all_gather | solution.py:21
  35.7 2.9 %copy.12 = bf16[1024,1024]{0,1:T(8,128)(2,1)S(1)} copy(bf16[1024,1024]{1,0:T(8,128)(2,1)} %param.4) | data formatting | bytes 4194304 | tf_op args[0]
  38.6 0.8 convert_bitcast_fusion.1
  39.3 2.5 %copy.13 = bf16[1024,64,16]{0,2,1:T(8,128)(2,1)} copy(bf16[1024,64,16]{0,1,2:T(8,128)(2,1)S(1)} %convert_bitcast_fusion.1) | data formatting | bytes 4194304 | tf_op jit(solution)/shard_map/convert_element_type | solution.py:26
  41.8 4.5 %all-to-all-start = ((bf16[1024,4,256]{0,2,1:T(8,128)(2,1)}), bf16[1024,4,256]{0,2,1:T(8,128)(2,1)}, u32[]{:S(2)}, u32[]{:S(2)}) async-start(bf16[1024,4,256]{0,2,1:T(8,128)(2,1)} %bitcast.86), calls=%async_computation | async-start | bytes 4194304 | tf_op jit(solution)/shard_map/all_to_all | solution.py:28
  46.3 0.0 copy-start.1
  46.3 4.1 %copy.15 = f32[1024,1024]{0,1:T(8,128)} copy(bf16[1024,1024]{1,0:T(8,128)(2,1)} %param.7) | data formatting | bytes 6291456 | tf_op jit(solution)/shard_map/convert_element_type | solution.py:37
  50.4 0.0 copy-done.1
  50.4 26.4 %all_gather.7 = bf16[16,64,64]{2,1,0:T(8,128)(2,1)S(1)} all-gather(bf16[16,8,64]{2,1,0:T(8,128)(2,1)S(1)} %copy-done.1), channel_id=1, replica_groups=mesh['dp'=8,'mp'=4] {'dp'}, dimensions={1}, use_global_device_ids=true | all-gather | bytes 147456 | tf_op jit(solution)/shard_map/all_gather | solution.py:22
  76.9 0.0 all-to-all-done
  76.9 13.7 %fusion.8 = (bf16[1024,16,64]{0,2,1:T(8,128)(2,1)S(1)}, bf16[1024,16,64]{0,2,1:T(8,128)(2,1)}) fusion(f32[1024,16,64]{0,2,1:T(8,128)} %bitcast.87, bf16[1024,4,16,16]{0,3,2,1:T(8,128)(2,1)} %bitcast.3, bf16[16,4,16,64]{3,2,1,0:T(8,128)(2,1)S(1)} %bitcast.89), kind=kOutput, calls=%fused_computation.10 | convolution fusion | flops 212860928 | bytes 10616832 | tf_op jit(solution)/shard_map/tpmj,mpjn->tmn/dot_general | solution.py:31
  90.5 0.0 copy-start
  90.5 0.7 convert_bitcast_fusion
  91.2 1.5 copy.16
  92.7 0.0 copy-done
  92.7 4.4 %all-to-all-start.1 = ((bf16[1024,4,256]{0,2,1:T(8,128)(2,1)}), bf16[1024,4,256]{0,2,1:T(8,128)(2,1)}, u32[]{:S(2)}, u32[]{:S(2)}) async-start(bf16[1024,4,256]{0,2,1:T(8,128)(2,1)} %bitcast.85), calls=%async_computation.1 | async-start | bytes 4194304 | tf_op jit(solution)/shard_map/all_to_all | solution.py:44
  97.2 0.0 reduce-scatter.5.cloned.1.call-start
  97.2 3.8 %fusion.23 = f32[16,4,16,64]{3,2,1,0:T(8,128)} fusion(bf16[1024,16,64]{0,2,1:T(8,128)(2,1)} %copy-done, bf16[1024,4,16,16]{0,3,2,1:T(8,128)(2,1)} %bitcast.3), kind=kOutput, calls=%fused_computation.34 | convolution fusion | flops 134217728 | bytes 4456448 | tf_op jit(solution)/shard_map/tpmj,tmn->mpjn/dot_general | solution.py:40
  101.0 0.0 reduce-scatter.5.cloned.1.call-update
  101.0 0.0 reduce-scatter.3.cloned.1.call-start
  101.1 21.9 %all-to-all-done.1 = bf16[1024,4,256]{0,2,1:T(8,128)(2,1)} async-done(((bf16[1024,4,256]{0,2,1:T(8,128)(2,1)}), bf16[1024,4,256]{0,2,1:T(8,128)(2,1)}, u32[]{:S(2)}, u32[]{:S(2)}) %all-to-all-start.1) | async-done | bytes 2097184 | tf_op jit(solution)/shard_map/all_to_all | solution.py:44
  122.9 3.1 %fusion.28 = f32[16,4,16,64]{3,2,1,0:T(8,128)S(1)} fusion(bf16[1024,16,64,1]{0,2,3,1:T(8,128)(2,1)S(1)} %bitcast.84, bf16[1024,4,16,16]{0,3,2,1:T(8,128)(2,1)} %bitcast.14), kind=kOutput, calls=%fused_computation.39 | convolution fusion | flops 134217728 | bytes 4456448 | tf_op jit(solution)/shard_map/tik,tqmi->ikqm/dot_general | solution.py:46
  126.0 1.0 copy.18
  127.0 0.0 reduce-scatter.3.cloned.1.call-update
  127.0 4.0 %copy.20 = bf16[1024,1024]{1,0:T(8,128)(2,1)} copy(bf16[1024,1024]{0,1:T(8,128)(2,1)} %bitcast.88) | data formatting | bytes 4194304
  131.0 32.4 %reduce-scatter.5.cloned.1.call-done = f32[16,8,64]{2,1,0:T(8,128)} async-done(((f32[16,64,64]{2,1,0:T(8,128)}), f32[16,8,64]{2,1,0:T(8,128)}) %reduce-scatter.5.cloned.1.call-update) | async-done | bytes 32784 | tf_op jit(solution)/shard_map/reduce_scatter | solution.py:50
  163.4 66.1 %reduce-scatter.3.cloned.1.call-done = f32[16,8,64]{2,1,0:T(8,128)} async-done(((f32[16,64,64]{2,1,0:T(8,128)}), f32[16,8,64]{2,1,0:T(8,128)}) %reduce-scatter.3.cloned.1.call-update) | async-done | bytes 32784 | tf_op jit(solution)/shard_map/reduce_scatter | solution.py:49
Async XLA Ops:
  41.8 35.0 %all-to-all-start = ((bf16[1024,4,256]{0,2,1:T(8,128)(2,1)}), bf16[1024,4,256]{0,2,1:T(8,128)(2,1)}, u32[]{:S(2)}, u32[]{:S(2)}) async-start(bf16[1024,4,256]{0,2,1:T(8,128)(2,1)} %bitcast.86), calls=%async_computation | async-start | bytes 4194304 | tf_op jit(solution)/shard_map/all_to_all | solution.py:28
  46.3 4.1 %copy-start.1 = (bf16[16,8,64]{2,1,0:T(8,128)(2,1)S(1)}, bf16[16,8,64]{2,1,0:T(8,128)(2,1)}, u32[]{:S(2)}) copy-start(bf16[16,8,64]{2,1,0:T(8,128)(2,1)} %param.6) | copy-start | bytes 49156
  90.5 2.2 copy-start
  92.7 30.2 %all-to-all-start.1 = ((bf16[1024,4,256]{0,2,1:T(8,128)(2,1)}), bf16[1024,4,256]{0,2,1:T(8,128)(2,1)}, u32[]{:S(2)}, u32[]{:S(2)}) async-start(bf16[1024,4,256]{0,2,1:T(8,128)(2,1)} %bitcast.85), calls=%async_computation.1 | async-start | bytes 4194304 | tf_op jit(solution)/shard_map/all_to_all | solution.py:44
  97.2 66.2 %reduce-scatter.5.cloned.1.call-start = ((), (), s32[]{:S(2)}) async-start(), calls=%async_computation.5 | async-start | bytes 589824 | tf_op jit(solution)/shard_map/reduce_scatter | solution.py:50
  101.0 128.5 %reduce-scatter.3.cloned.1.call-start = ((), (), s32[]{:S(2)}) async-start(), calls=%async_computation.4 | async-start | bytes 589824 | tf_op jit(solution)/shard_map/reduce_scatter | solution.py:49
Sparse Core Ops, SparseCore 0:
  101.9 61.4 reduce-scatter.4
  167.4 62.1 reduce-scatter.2
where the time goes:
time: 237 us; the launch traced here: 236 us
  waiting for transfers between devices  120 us (51%)
  blocking collectives  55 us (23%)
  matrix products  21.9 us (9%)
  local copies, waits for them, and re-layouts  15.9 us (7%)
  between operations  14.1 us (6%)
  starting transfers between devices  8.99 us (4%)
    reduce_scatter x1, waiting for transfers between devices, shards(): lax.psum_scatter(part_right, 'dp', scatter_dimension=1, tiled=True)  66.1 us
    reduce_scatter x1, waiting for transfers between devices, shards(): lax.psum_scatter(part_left, 'dp', scatter_dimension=1, tiled=True)  32.4 us
    all_gather x1, blocking collectives, shards(): lax.all_gather(right_weight, 'dp', axis=1, tiled=True)  28.6 us
    all_gather x1, blocking collectives, shards(): lax.all_gather(left_weight, 'dp', axis=1, tiled=True)  26.4 us
    all_to_all x1, waiting for transfers between devices, shards(): lax.all_to_all(dmixed, 'mp', split_axis=1, concat_axis=1, tiled=True)  21.9 us
    dot_general x1, matrix products, shards(): jnp.einsum('tpmj,mpjn->tmn', mixed, left_four, preferred_element_type=jnp...  13.7 us
    unnamed x6, local copies, waits for them, and re-layouts  6.83 us
  transfers between devices with their start and end apart: 4, of which 3 were waited for; matrix products, arithmetic and copies ran while one was open for 7% of the time, Pallas kernels for 0%

commit v1 on v0

--- a/solution.py
+++ b/solution.py
@@ -17,9 +17,13 @@
     tok_rows = tokens.shape[0]
     groups = lax.axis_size("mp")
     owned = NB // groups
+
+    def name_bands_now(payload):
+        return jnp.concatenate(lax.all_gather(payload, "dp"), axis=1)
+
     right_rows, left_rows = (
         lax.all_gather(right_weight, "dp", axis=1, tiled=True),
-        lax.all_gather(left_weight, "dp", axis=1, tiled=True),
+        name_bands_now(left_weight),
     )
     xs = tokens.reshape(tok_rows, owned, BS)
     inner = jnp.einsum("tik,ikm->tmi", xs, right_rows, preferred_element_type=jnp.float32)

time: 237 us -> 243 us (1.025)
  blocking collectives: 55 us -> 59.3 us
    all_gather x1, blocking collectives: 26.4 us -> 30.8 us  [name_bands_now(): return jnp.concatenate(lax.all_gather(payload, 'dp'), axis=1)]
where the time goes in v1:
time: 243 us; the launch traced here: 242 us
  waiting for transfers between devices  122 us (50%)
  blocking collectives  59.3 us (24%)
  matrix products  21.9 us (9%)
  local copies, waits for them, and re-layouts  16 us (7%)
  between operations  14.1 us (6%)
  starting transfers between devices  8.99 us (4%)
    reduce_scatter x1, waiting for transfers between devices, shards(): lax.psum_scatter(part_right, 'dp', scatter_dimension=1, tiled=True)  66.1 us
    reduce_scatter x1, waiting for transfers between devices, shards(): lax.psum_scatter(part_left, 'dp', scatter_dimension=1, tiled=True)  33.9 us
    all_gather x1, blocking collectives, name_bands_now(): return jnp.concatenate(lax.all_gather(payload, 'dp'), axis=1)  30.8 us
    all_gather x1, blocking collectives, shards(): lax.all_gather(right_weight, 'dp', axis=1, tiled=True)  28.6 us
    all_to_all x1, waiting for transfers between devices, shards(): lax.all_to_all(dmixed, 'mp', split_axis=1, concat_axis=1, tiled=True)  21.9 us
    dot_general x1, matrix products, shards(): jnp.einsum('tpmj,mpjn->tmn', mixed, left_four, preferred_element_type=jnp...  13.7 us
    unnamed x6, local copies, waits for them, and re-layouts  6.82 us
  transfers between devices with their start and end apart: 4, of which 3 were waited for; matrix products, arithmetic and copies ran while one was open for 7% of the time, Pallas kernels for 0%

profile of v1, /device:TPU:0, one launch (start us, length us, event | category | flops | bytes accessed | tf_op | source)
XLA Modules:
  0.0 242.3 jit_solution(14853187780677237730)
XLA Ops:
  7.2 28.6 %all_gather.9 = bf16[16,64,64]{2,1,0:T(8,128)(2,1)S(1)} all-gather(bf16[16,8,64]{2,1,0:T(8,128)(2,1)} %param.5), channel_id=1, replica_groups=mesh['dp'=8,'mp'=4] {'dp'}, dimensions={1}, use_global_device_ids=true | all-gather | bytes 147456 | tf_op jit(solution)/shard_map/all_gather | solution.py:25
  35.7 2.9 %copy.41 = bf16[1024,1024]{0,1:T(8,128)(2,1)S(1)} copy(bf16[1024,1024]{1,0:T(8,128)(2,1)} %param.4) | data formatting | bytes 4194304 | tf_op args[0]
  38.6 0.8 convert_bitcast_fusion.1
  39.3 0.0 copy-start.1
  39.4 2.5 %copy.42 = bf16[1024,64,16]{0,2,1:T(8,128)(2,1)} copy(bf16[1024,64,16]{0,1,2:T(8,128)(2,1)S(1)} %convert_bitcast_fusion.1) | data formatting | bytes 4194304 | tf_op jit(solution)/shard_map/convert_element_type | solution.py:30
  41.8 4.5 %all-to-all-start = ((bf16[1024,4,256]{0,2,1:T(8,128)(2,1)}), bf16[1024,4,256]{0,2,1:T(8,128)(2,1)}, u32[]{:S(2)}, u32[]{:S(2)}) async-start(bf16[1024,4,256]{0,2,1:T(8,128)(2,1)} %bitcast.89), calls=%async_computation | async-start | bytes 4194304 | tf_op jit(solution)/shard_map/all_to_all | solution.py:32
  46.3 0.0 copy-done.1
  46.3 30.8 %all-gather = bf16[128,8,64]{2,1,0:T(8,128)(2,1)S(1)} all-gather(bf16[16,8,64]{2,1,0:T(8,128)(2,1)S(1)} %copy-done.1), channel_id=2, replica_groups=mesh['dp'=8,'mp'=4] {'dp'}, dimensions={0}, use_global_device_ids=true | all-gather | bytes 147456 | tf_op jit(solution)/shard_map/all_gather | solution.py:22
  77.1 0.1 copy.43
  77.1 4.1 %copy.45 = f32[1024,1024]{0,1:T(8,128)} copy(bf16[1024,1024]{1,0:T(8,128)(2,1)} %param.7) | data formatting | bytes 6291456 | tf_op jit(solution)/shard_map/convert_element_type | solution.py:41
  81.3 0.0 all-to-all-done
  81.3 13.7 %fusion.8 = (bf16[1024,16,64]{0,2,1:T(8,128)(2,1)S(1)}, bf16[1024,16,64]{0,2,1:T(8,128)(2,1)}) fusion(f32[1024,16,64]{0,2,1:T(8,128)} %bitcast.90, bf16[1024,4,16,16]{0,3,2,1:T(8,128)(2,1)} %bitcast.3, bf16[16,4,16,64]{3,2,1,0:T(8,128)(2,1)S(1)} %bitcast.92), kind=kOutput, calls=%fused_computation.10 | convolution fusion | flops 212860928 | bytes 10616832 | tf_op jit(solution)/shard_map/tpmj,mpjn->tmn/dot_general | solution.py:35
  95.0 0.0 copy-start
  95.0 0.7 convert_bitcast_fusion
  95.7 1.5 copy.46
  97.1 0.0 copy-done
  97.2 4.4 %all-to-all-start.1 = ((bf16[1024,4,256]{0,2,1:T(8,128)(2,1)}), bf16[1024,4,256]{0,2,1:T(8,128)(2,1)}, u32[]{:S(2)}, u32[]{:S(2)}) async-start(bf16[1024,4,256]{0,2,1:T(8,128)(2,1)} %bitcast.88), calls=%async_computation.1 | async-start | bytes 4194304 | tf_op jit(solution)/shard_map/all_to_all | solution.py:48
  101.6 0.0 reduce-scatter.5.cloned.1.call-start
  101.7 3.8 %fusion.23 = f32[16,4,16,64]{3,2,1,0:T(8,128)} fusion(bf16[1024,16,64]{0,2,1:T(8,128)(2,1)} %copy-done, bf16[1024,4,16,16]{0,3,2,1:T(8,128)(2,1)} %bitcast.3), kind=kOutput, calls=%fused_computation.34 | convolution fusion | flops 134217728 | bytes 4456448 | tf_op jit(solution)/shard_map/tpmj,tmn->mpjn/dot_general | solution.py:44
  105.4 0.0 reduce-scatter.5.cloned.1.call-update
  105.4 0.0 reduce-scatter.3.cloned.1.call-start
  105.5 21.9 %all-to-all-done.1 = bf16[1024,4,256]{0,2,1:T(8,128)(2,1)} async-done(((bf16[1024,4,256]{0,2,1:T(8,128)(2,1)}), bf16[1024,4,256]{0,2,1:T(8,128)(2,1)}, u32[]{:S(2)}, u32[]{:S(2)}) %all-to-all-start.1) | async-done | bytes 2097184 | tf_op jit(solution)/shard_map/all_to_all | solution.py:48
  127.3 3.1 %fusion.28 = f32[16,4,16,64]{3,2,1,0:T(8,128)S(1)} fusion(bf16[1024,16,64,1]{0,2,3,1:T(8,128)(2,1)S(1)} %bitcast.87, bf16[1024,4,16,16]{0,3,2,1:T(8,128)(2,1)} %bitcast.16), kind=kOutput, calls=%fused_computation.39 | convolution fusion | flops 134217728 | bytes 4456448 | tf_op jit(solution)/shard_map/tik,tqmi->ikqm/dot_general | solution.py:50
  130.4 1.0 copy.48
  131.4 0.0 reduce-scatter.3.cloned.1.call-update
  131.4 4.0 %copy.50 = bf16[1024,1024]{1,0:T(8,128)(2,1)} copy(bf16[1024,1024]{0,1:T(8,128)(2,1)} %bitcast.91) | data formatting | bytes 4194304
  135.4 33.9 %reduce-scatter.5.cloned.1.call-done = f32[16,8,64]{2,1,0:T(8,128)} async-done(((f32[16,64,64]{2,1,0:T(8,128)}), f32[16,8,64]{2,1,0:T(8,128)}) %reduce-scatter.5.cloned.1.call-update) | async-done | bytes 32784 | tf_op jit(solution)/shard_map/reduce_scatter | solution.py:54
  169.3 66.1 %reduce-scatter.3.cloned.1.call-done = f32[16,8,64]{2,1,0:T(8,128)} async-done(((f32[16,64,64]{2,1,0:T(8,128)}), f32[16,8,64]{2,1,0:T(8,128)}) %reduce-scatter.3.cloned.1.call-update) | async-done | bytes 32784 | tf_op jit(solution)/shard_map/reduce_scatter | solution.py:53
Async XLA Ops:
  39.3 7.0 %copy-start.1 = (bf16[16,8,64]{2,1,0:T(8,128)(2,1)S(1)}, bf16[16,8,64]{2,1,0:T(8,128)(2,1)}, u32[]{:S(2)}) copy-start(bf16[16,8,64]{2,1,0:T(8,128)(2,1)} %param.6) | copy-start | bytes 49156
  41.8 39.4 %all-to-all-start = ((bf16[1024,4,256]{0,2,1:T(8,128)(2,1)}), bf16[1024,4,256]{0,2,1:T(8,128)(2,1)}, u32[]{:S(2)}, u32[]{:S(2)}) async-start(bf16[1024,4,256]{0,2,1:T(8,128)(2,1)} %bitcast.89), calls=%async_computation | async-start | bytes 4194304 | tf_op jit(solution)/shard_map/all_to_all | solution.py:32
  95.0 2.2 copy-start
  97.2 30.2 %all-to-all-start.1 = ((bf16[1024,4,256]{0,2,1:T(8,128)(2,1)}), bf16[1024,4,256]{0,2,1:T(8,128)(2,1)}, u32[]{:S(2)}, u32[]{:S(2)}) async-start(bf16[1024,4,256]{0,2,1:T(8,128)(2,1)} %bitcast.88), calls=%async_computation.1 | async-start | bytes 4194304 | tf_op jit(solution)/shard_map/all_to_all | solution.py:48
  101.6 67.7 %reduce-scatter.5.cloned.1.call-start = ((), (), s32[]{:S(2)}) async-start(), calls=%async_computation.5 | async-start | bytes 589824 | tf_op jit(solution)/shard_map/reduce_scatter | solution.py:54
  105.4 130.0 %reduce-scatter.3.cloned.1.call-start = ((), (), s32[]{:S(2)}) async-start(), calls=%async_computation.4 | async-start | bytes 589824 | tf_op jit(solution)/shard_map/reduce_scatter | solution.py:53
Sparse Core Ops, SparseCore 0:
  106.3 62.9 reduce-scatter.4
  173.2 62.1 reduce-scatter.2
